TPU v7x, 32 devices: a whole 2x2x4 slice. The times are simulated.
32 devices in a mesh: dp: 8 (over z, x), mp: 4 (over y, core).
Axes of the slice: x: 2, y: 2, z: 4, core: 2. Of those that a mesh axis runs over, the one named last changes fastest.
Arguments:
- grads: bfloat16 [8, 4, 4096, 256], P('dp', 'mp'), may hold values from -6 to 6
- master: float32 [4, 4096, 256], P('mp', 'dp'), may hold values from -6 to 6
- m_codes: bfloat16 [4, 4096, 256], P('mp', 'dp'), may hold values from -1 to 1
- m_scale: float32 [4, 4096], P('mp', 'dp'), may hold values from 0.005 to 0.05
- v_codes: bfloat16 [4, 4096, 256], P('mp', 'dp'), may hold values from 0.049804688 to 1
- v_scale: float32 [4, 4096], P('mp', 'dp'), may hold values from 0.001 to 0.01
Outputs:
- master_out: float32 [4, 4096, 256], P('mp', 'dp')
- m_codes_out: bfloat16 [4, 4096, 256], P('mp', 'dp')
- m_scale_out: float32 [4, 4096], P('mp', 'dp')
- v_codes_out: bfloat16 [4, 4096, 256], P('mp', 'dp')
- v_scale_out: float32 [4, 4096], P('mp', 'dp')
- weights: bfloat16 [4, 4096, 256], P('mp')
All inputs are finite; a program needn't handle non-finite values. Where the computation divides by a largest or mean magnitude, that divisor is 1e-20 or more.
Results may differ from a plain program's by a relative error of at most 0.024.
Values may be sent and summed in bfloat16 or wider, within the bound.
A program may use at most 128 MiB of HBM per device.

v0:
```python
import functools
import math

import jax
import jax.numpy as jnp
from jax import lax
from jax.experimental import pallas as pl
from jax.experimental.pallas import tpu as pltpu
from jax.sharding import PartitionSpec as P

STEP = 8
LANES = 128
VMEM_ALL = 67043328
VMEM_GRANT = 60 * 1024 * 1024
MESH = pl.DeviceIdType.MESH

LINE, HALF, DIRECT = 0, 1, 2
ACROSS, SUM, CROSS, UPDATE, SPREAD, PASS, OVER = range(7)
CHUNK = 64
PLANS = {}


def unpacked(codes):
    return [
        (c // 100000, c // 1000 % 100, c // 100 % 10, c // 10 % 10, c % 10) for c in codes
    ]


PLANS[4] = (
    (1, 1, 1, 1, 1, 1, 1, 1),
    ((0, LINE), (0, LINE), (0, LINE), (1, HALF), (0, LINE), (0, LINE), (0, LINE), (0, LINE)),
    ((1, LINE), (0, HALF), (0, HALF), (0, LINE), (1, LINE), (0, LINE), (0, LINE), (0, LINE)),
    (
        unpacked((
            30, 1030, 103010, 103021, 103020, 6030, 103031, 4030, 20, 103030, 1020, 103011, 5030, 100030,
            2030, 101030, 6020, 7030, 104030, 4020, 100020, 10, 101020, 106030, 105030, 5020, 203000, 0,
            106020, 1010, 107030, 2020, 104020, 102030, 6010, 100010, 1000, 303000, 7020, 105020, 4010, 6000,
            101010, 4000, 102020, 300000, 5010, 106010, 2010, 301000, 5000, 107020, 7010, 104010, 2000, 7000,
            304000, 306000, 105010, 102010, 603110, 305000, 107010, 601110, 302000, 603130, 307000, 606120, 606110, 400000,
            601130, 404000, 605110, 606130, 605120, 605130, 602120, 603120, 602130, 601120, 602110, 607130, 607120, 607110,
        )),
        unpacked((
            30, 1030, 103110, 103111, 6030, 4030, 0, 20, 5030, 1000, 103011, 10, 103010, 1020,
            103021, 103020, 2030, 203000, 6000, 101020, 6020, 100020, 1010, 104020, 7030, 100010, 4000, 101010,
            303000, 101110, 4020, 105020, 100110, 6010, 106020, 4010, 106010, 5000, 5020, 107020, 503110, 2000,
            300000, 104110, 2020, 102020, 104010, 106110, 5010, 7000, 503010, 7020, 301000, 105110, 500110, 2010,
            105010, 7010, 102110, 306000, 500010, 102010, 503120, 603110, 501110, 304000, 107110, 107010, 506110, 606110,
            506010, 606010, 603010, 305000, 500120, 302000, 501120, 601110, 505010, 605010, 307000, 506120, 504010, 601010,
            505110, 605110, 505120, 602010, 502110, 602110, 507010, 502120, 400000, 504120, 606120, 500011, 507110, 504011,
            602120, 507120, 605120, 500111, 603120, 404000, 500121, 601120, 504121, 607010, 607110, 504110, 504111, 607120,
        )),
        unpacked((
            0, 1000, 103010, 103011, 6000, 4000, 30, 10, 5000, 1030, 103111, 20, 103110, 1010,
            103121, 103120, 2000, 203000, 6030, 101120, 6010, 100120, 1020, 104120, 7000, 100110, 4030, 101110,
            303000, 101010, 4010, 105120, 100010, 6020, 106120, 4020, 106110, 5030, 5010, 107120, 503010, 2030,
            300000, 104010, 2010, 102120, 104110, 106010, 5020, 7030, 503110, 7010, 301000, 105010, 500010, 2020,
            105110, 7020, 102010, 306000, 500110, 102110, 503020, 603010, 501010, 304000, 107010, 107110, 506010, 606010,
            506110, 606110, 603110, 305000, 500020, 302000, 501020, 601010, 505110, 605110, 307000, 506020, 504110, 601110,
            505010, 605010, 505020, 602110, 502010, 602010, 507110, 502020, 400000, 504020, 606020, 500111, 507010, 504111,
            602020, 507020, 605020, 500011, 603020, 404000, 500021, 601020, 504021, 607110, 607010, 504010, 504011, 607020,
        )),
        unpacked((
            0, 1000, 103110, 103121, 103120, 6000, 103131, 4000, 10, 103130, 1010, 103111, 5000, 100130,
            2000, 101130, 6010, 7000, 104130, 4010, 100120, 20, 101120, 106130, 105130, 5010, 203000, 30,
            106120, 1020, 107130, 2010, 104120, 102130, 6020, 100110, 1030, 303000, 7010, 105120, 4020, 6030,
            101110, 4030, 102120, 300000, 5020, 106110, 2020, 301000, 5030, 107120, 7020, 104110, 2030, 7030,
            304000, 306000, 105110, 102110, 603010, 305000, 107110, 601010, 302000, 603030, 307000, 606020, 606010, 400000,
            601030, 404000, 605010, 606030, 605020, 605030, 602020, 603020, 602030, 601020, 602010, 607030, 607020, 607010,
        )),
    ),
)


def plan_for(outer, owned):
    if outer in PLANS:
        parts, sums, spreads, orders = PLANS[outer]
        unit = owned // sum(parts)
        if unit * sum(parts) == owned and unit % 16 == 0:
            return [unit * part for part in parts], sums, spreads, orders
    orders = []
    for z in range(outer):
        order = [(ACROSS, 0, 0, (z + 1 + step) % outer, 0) for step in range(outer)]
        for distance in range(outer - 1, 0, -1):
            order += [
                (SUM, 0, left, distance, 0) for left in (0, 1)
                if (z - distance >= 0 if left else z + distance < outer)
            ]
        order.append((UPDATE, 0, 0, 0, 0))
        for distance in range(1, outer):
            for left in (0, 1):
                if z + distance < outer if left else z - distance >= 0:
                    if z > 0 if left else z < outer - 1:
                        order.append((PASS, 0, left, distance, 0))
                    order.append((OVER, 0, left, distance, 0))
        orders.append(order)
    return [owned], [(0, LINE)], [(0, LINE)], orders


def kernel(
    outer, plan, grads, master, m_codes, m_scale, v_codes, v_scale,
    master_new, m_new, ms_new, v_new, vs_new, weights,
    own, xgot, stage, right_got, left_got, ms_wide, vs_wide,
    master_in, m_in, v_in, ms_in, vs_in,
    own_sem, state_sem,
    x_send, x_recv, sum_send, right_recv, left_recv, first_send, pass_send, w_recv, a_send, a_recv,
):
    sizes, sums, spreads, orders = plan
    pieces = len(sizes)
    starts = [sum(sizes[:k]) for k in range(pieces)]
    owned, width = master.shape[1], master.shape[2]
    replicas = 2 * outer
    f32, bf16 = jnp.float32, jnp.bfloat16
    me = lax.axis_index("dp")
    x = lax.rem(me, 2)
    place = lax.div(me, 2)
    other = place * 2 + 1 - x

    barrier = pltpu.get_barrier_semaphore()
    pl.semaphore_signal(barrier, inc=1, device_id={"dp": other}, device_id_type=MESH)
    for step in range(1, outer):
        pl.semaphore_signal(
            barrier, inc=1, device_id={"dp": lax.rem(place + step, outer) * 2 + x}, device_id_type=MESH
        )

    def rows_in(k):
        return pl.ds(starts[k], sizes[k])

    own_copies = [
        pltpu.make_async_copy(grads.at[:, rows_in(k), :], own.at[:, rows_in(k), :], own_sem.at[k])
        for k in range(pieces)
    ]
    scale_copies = [
        pltpu.make_async_copy(m_scale, ms_in, state_sem.at[3]),
        pltpu.make_async_copy(v_scale, vs_in, state_sem.at[4]),
    ]
    state_copies = [
        pltpu.make_async_copy(src, dst, state_sem.at[i])
        for i, (src, dst) in enumerate(((master, master_in), (m_codes, m_in), (v_codes, v_in)))
    ]
    for copy in own_copies + scale_copies + state_copies:
        copy.start()
    for copy in scale_copies:
        copy.wait()
    for source, wide in ((ms_in, ms_wide), (vs_in, vs_wide)):
        for c in range(owned // LANES):
            span = pl.ds(c * LANES, LANES)
            wide[span, :] = jnp.transpose(jnp.broadcast_to(source[0:1, span], (LANES, LANES)))
    for copy in own_copies + state_copies:
        copy.wait()
    pl.semaphore_wait(barrier, outer)

    def remote(src, dst, send, recv, device):
        return pltpu.make_async_remote_copy(
            src_ref=src, dst_ref=dst, send_sem=send, recv_sem=recv,
            device_id={"dp": device}, device_id_type=MESH,
        )

    def column(block):
        return 1 - x if block else x

    def in_rows(k, body):
        chunk = min(CHUNK, sizes[k])
        count = sizes[k] // chunk
        if count <= 2 and count * chunk == sizes[k]:
            for c in range(count):
                body(pl.ds(starts[k] + c * chunk, chunk))
        elif count * chunk == sizes[k]:
            lax.fori_loop(
                0, count, lambda c, _: body(pl.ds(pl.multiple_of(starts[k] + c * chunk, 16), chunk)), None
            )
        else:
            body(rows_in(k))

    def program(z):
        started = []
        taken = set()

        def launch(copy):
            copy.start()
            started.append(copy)

        def seat(left):
            return outer - 1 - z if left else z

        def at(left, number):
            return outer - 1 - number if left else number

        def x_copy(k, t, src):
            return remote(src, xgot.at[t, rows_in(k), :], x_send.at[k, t], x_recv.at[k, t], other)

        def x_wait(k, t):
            x_copy(k, t, xgot.at[t, rows_in(k), :]).wait_recv()

        def across(k, t):
            launch(x_copy(k, t, own.at[t * 2 + 1 - x, rows_in(k), :]))

        def got_of(left):
            return (left_got, left_recv) if left else (right_got, right_recv)

        def sum_wait(k, left, slot, block):
            got, recv = got_of(left)
            ref = got.at[slot, block, rows_in(k), :]
            remote(ref, ref, sum_send.at[k, slot, block], recv.at[k, slot, block], other).wait_recv()

        def add_up(k, t, block, terms, rows):
            total = own[t * 2 + column(block), rows, :].astype(f32)
            if not sums[k][0]:
                total = total + xgot[t, rows, :].astype(f32)
            for left, slot in terms:
                total = total + got_of(left)[0][slot, block, rows, :].astype(f32)
            return total

        def partial_sum(k, left, distance, block):
            z_first, form = sums[k]
            got, recv = got_of(left)
            seated = seat(left)
            t = at(left, seated + distance)
            adds = form == LINE and seated > 0 or form == HALF and seated == 1
            hops = form == LINE or form == HALF and seated == 0
            slot = t if hops else z
            dest = at(left, seated + 1) if hops else t
            if z_first and not adds:
                src = own.at[t * 2 + column(block), rows_in(k), :]
            else:
                if not z_first:
                    x_wait(k, t)
                if adds:
                    sum_wait(k, left, t, block)

                def body(rows):
                    total = add_up(k, t, block, [(left, t)] if adds else [], rows)
                    stage[t, block, rows, :] = total.astype(bf16)
                in_rows(k, body)
                src = stage.at[t, block, rows_in(k), :]
            launch(remote(
                src, got.at[slot, block, rows_in(k), :], sum_send.at[k, t, block],
                recv.at[k, slot, block], dest * 2 + x,
            ))

        def arrived(k, block):
            form = sums[k][1]
            terms = []
            for left in (0, 1):
                seated = seat(left)
                if seated == 0:
                    continue
                if form == LINE or form == HALF and seated == 1:
                    terms.append((left, z))
                else:
                    terms += [(left, at(left, s)) for s in range(1 if form == HALF else 0, seated)]
            if not sums[k][0]:
                x_wait(k, z)
            for left, slot in terms:
                sum_wait(k, left, slot, block)
            return terms

        def cross(k):
            terms = arrived(k, 1)

            def body(rows):
                stage[z, 1, rows, :] = add_up(k, z, 1, terms, rows).astype(bf16)
            in_rows(k, body)
            launch(x_copy(k, z, stage.at[z, 1, rows_in(k), :]))

        def weight_rows(k, source, block):
            start = (source * 2 + column(block)) * owned + starts[k]
            return weights.at[0, pl.ds(pl.multiple_of(start, 16), sizes[k]), :]

        def weight_copy(k, source, block, send, dest):
            rows = weight_rows(k, source, block)
            return remote(rows, rows, send, w_recv.at[k, source, block], dest * 2 + x)

        def weight_wait(k, source, block):
            if (k, source, block) not in taken:
                taken.add((k, source, block))
                weight_copy(k, source, block, pass_send.at[k, source, block], z).wait_recv()

        def weight_over(k, source):
            rows = weight_rows(k, source, 0)
            return remote(rows, rows, a_send.at[k, source], a_recv.at[k, source], other)

        def first_sends(k, block):
            form = spreads[k][1]
            for left in (0, 1):
                seated = seat(left)
                last = outer - 1
                if seated == last:
                    continue
                if form == LINE or form == HALF and seated == last - 1:
                    dests = [seated + 1]
                else:
                    dests = range(last if form == DIRECT else last - 1, seated, -1)
                for number in dests:
                    dest = at(left, number)
                    launch(weight_copy(k, z, block, first_send.at[k, dest, block], dest))

        def update(k):
            terms = arrived(k, 0)
            if sums[k][0]:
                x_wait(k, z)
            repeat = width // LANES
            first_fix = 1.0 - 0.9**STEP
            second_fix = 1.0 - 0.95**STEP

            def body(rows):
                value = add_up(k, z, 0, terms, rows)
                if sums[k][0]:
                    value = value + xgot[z, rows, :].astype(f32)
                mean = value * (1.0 / replicas)
                ms = jnp.concatenate([ms_wide[rows, :]] * repeat, axis=1)
                vs = jnp.concatenate([vs_wide[rows, :]] * repeat, axis=1)
                one = 0.9 * m_in[0, rows].astype(f32) * ms + 0.1 * mean
                two = 0.95 * v_in[0, rows].astype(f32) * vs + 0.05 * mean * mean
                new = master_in[0, rows] - (0.1 / first_fix) * one / (
                    jnp.sqrt(two * (1.0 / second_fix)) + 1e-08
                )
                mine = pl.ds(pl.multiple_of(me * owned + rows.start, 16), rows.size)
                weights[0, mine, :] = new.astype(bf16)
                master_new[0, rows] = new
                one_top = jnp.max(jnp.abs(one), axis=-1, keepdims=True) + 1e-06
                two_top = jnp.max(jnp.abs(two), axis=-1, keepdims=True) + 1e-06
                m_new[0, rows] = (one / one_top).astype(bf16)
                v_new[0, rows] = (two / two_top).astype(bf16)
                ms_wide[rows, :] = jnp.broadcast_to(one_top, (rows.size, LANES))
                vs_wide[rows, :] = jnp.broadcast_to(two_top, (rows.size, LANES))
            in_rows(k, body)
            if spreads[k][0]:
                launch(weight_over(k, z))
            first_sends(k, 0)
            if not spreads[k][0]:
                launch(weight_over(k, z))

        def spread(k):
            weight_over(k, z).wait_recv()
            first_sends(k, 1)

        def pass_on(k, left, apart, block):
            source = at(left, seat(left) - apart)
            weight_wait(k, source, block)
            launch(weight_copy(
                k, source, block, pass_send.at[k, source, block], at(left, seat(left) + 1)
            ))

        def over(k, left, apart):
            source = at(left, seat(left) - apart)
            weight_wait(k, source, 0)
            launch(weight_over(k, source))

        for kind, k, left, distance, block in orders[z]:
            if kind == ACROSS:
                across(k, distance)
            elif kind == SUM:
                partial_sum(k, left, distance, block)
            elif kind == CROSS:
                cross(k)
            elif kind == UPDATE:
                update(k)
            elif kind == SPREAD:
                spread(k)
            elif kind == PASS:
                pass_on(k, left, distance, block)
            else:
                over(k, left, distance)
        for wide, out in ((ms_wide, ms_new), (vs_wide, vs_new)):
            for c in range(owned // LANES):
                span = pl.ds(c * LANES, LANES)
                out[0:1, span] = jnp.transpose(wide[span, :])[0:1, :]
        for copy in started:
            copy.wait_send()
        for k in range(pieces):
            for source in range(outer):
                for block in range(1 + spreads[k][0]):
                    if source != z:
                        weight_wait(k, source, block)
                if not spreads[k][0]:
                    weight_over(k, source).wait_recv()

    for z in range(outer):
        pl.when(place == z)(functools.partial(program, z))


def write_out(*refs):
    sem = refs[-1]
    half = (len(refs) - 1) // 2
    copies = [
        pltpu.make_async_copy(refs[i], refs[half + i], sem.at[i]) for i in range(half)
    ]
    for copy in copies[::-1]:
        copy.start()
    for copy in copies:
        copy.wait()


def per_device(grads, master, m_codes, m_scale, v_codes, v_scale):
    outer = lax.axis_size("dp") // 2
    _, owned, width = master.shape
    plan = plan_for(outer, owned)
    sizes, sums, spreads, _ = plan
    pieces = len(sizes)
    blocks = 1 + max(kind[0] for kind in (*sums, *spreads))
    bf16, f32 = jnp.bfloat16, jnp.float32
    dma = pltpu.SemaphoreType.DMA
    shape = jax.ShapeDtypeStruct
    state = (1, owned, width)
    out_shapes = (
        (state, f32), (state, bf16), ((1, owned), f32),
        (state, bf16), ((1, owned), f32),
        ((1, 2 * outer * owned, width), bf16),
    )
    kept = sum(math.prod(dims) * jnp.dtype(kind).itemsize for dims, kind in out_shapes)
    outs = pl.pallas_call(
        functools.partial(kernel, outer, plan),
        out_shape=tuple(pltpu.VMEM(*each) for each in out_shapes),
        in_specs=[pl.BlockSpec(memory_space=pltpu.HBM)] * 6,
        out_specs=[pl.BlockSpec(memory_space=pltpu.VMEM)] * 6,
        scratch_shapes=[
            pltpu.VMEM((2 * outer, owned, width), bf16),
            pltpu.VMEM((outer, owned, width), bf16),
            pltpu.VMEM((outer, blocks, owned, width), bf16),
            pltpu.VMEM((outer, blocks, owned, width), bf16),
            pltpu.VMEM((outer, blocks, owned, width), bf16),
            pltpu.VMEM((owned, LANES), f32), pltpu.VMEM((owned, LANES), f32),
            pltpu.VMEM(state, f32), pltpu.VMEM(state, bf16), pltpu.VMEM(state, bf16),
            pltpu.VMEM((1, owned), f32), pltpu.VMEM((1, owned), f32),
            dma((pieces,)), dma((5,)),
            dma((pieces, outer)), dma((pieces, outer)),
            dma((pieces, outer, blocks)), dma((pieces, outer, blocks)), dma((pieces, outer, blocks)),
            dma((pieces, outer, blocks)), dma((pieces, outer, blocks)), dma((pieces, outer, blocks)),
            dma((pieces, outer)), dma((pieces, outer)),
        ],
        compiler_params=pltpu.CompilerParams(
            collective_id=0, has_side_effects=True,
            vmem_limit_bytes=min(VMEM_GRANT, VMEM_ALL - kept - 2**18),
        ),
    )(grads.reshape(2 * outer, owned, width), master, m_codes, m_scale, v_codes, v_scale)
    return tuple(pl.pallas_call(
        write_out,
        out_shape=tuple(shape(*each) for each in out_shapes),
        in_specs=[pl.BlockSpec(memory_space=pltpu.VMEM)] * 6,
        out_specs=[pl.BlockSpec(memory_space=pl.ANY)] * 6,
        scratch_shapes=[dma((6,))],
        compiler_params=pltpu.CompilerParams(vmem_limit_bytes=2**20),
    )(*[pltpu.with_memory_space_constraint(o, pltpu.VMEM) for o in outs]))


def solution(mesh):
    return jax.shard_map(
        per_device,
        mesh=mesh,
        in_specs=(
            P("dp", "mp", None, None),
            P("mp", "dp", None),
            P("mp", "dp", None),
            P("mp", "dp"),
            P("mp", "dp", None),
            P("mp", "dp"),
        ),
        out_specs=(
            P("mp", "dp", None),
            P("mp", "dp", None),
            P("mp", "dp"),
            P("mp", "dp", None),
            P("mp", "dp"),
            P("mp", None, None),
        ),
        check_vma=False,
    )
```

profile of v0, /device:TPU:0, one launch (start us, length us, event | category | flops | bytes accessed | tf_op | source)
XLA Modules:
  0.0 53.5 jit_solution(2601415657850685110)
XLA Ops:
  0.6 51.1 %shard_map.109 = (f32[1,512,256]{2,1,0:T(8,128)S(1)}, bf16[1,512,256]{2,1,0:T(8,128)(2,1)S(1)}, f32[1,512]{1,0:T(1,128)S(1)}, bf16[1,512,256]{2,1,0:T(8,128)(2,1...) custom-call(bf16[8,512,256]{2,1,0:T(8,128)(2,1)} %bitcast.1, f32[1,512,256]{2,1,0:T(8,128)} %master.1, ...), custom_call_target="tpu_custom_call" | custom-call | tf_op jit(solution)/shard_map/pallas_call | solution.py:411
  51.8 1.7 %shard_map.110 = (f32[1,512,256]{2,1,0:T(8,128)}, bf16[1,512,256]{2,1,0:T(8,128)(2,1)}, f32[1,512]{1,0:T(1,128)}, bf16[1,512,256]{2,1,0:T(8,128)(2,1)}, f32[1,512]{1,0:T(1,128)}, /*index=5*/bf16[1,4096,256]{2,1,0:T(8,128)(2,1)}) custom-call(f32[1,512,256]{2,1,0:T(8,128)S(1)} %get-tuple-element.12.refs_0_, ...), custom_call_target="tpu_custom_call" | custom-call | tf_op jit(solution)/shard_map/pallas_call | solution.py:436
where the time goes:
time: 53.6 us; the launch traced here: 53.5 us
  Pallas kernels  52.9 us (99%)
  between operations  0.64 us (1%)
    pallas_call x1, Pallas kernels, per_device(): pl.pallas_call(functools.partial(kernel, outer, plan), out_shape=tuple((p...  51.1 us
    pallas_call x1, Pallas kernels, per_device(): pl.pallas_call(write_out, out_shape=tuple((shape(*each) for each in out_s...  1.73 us

commit v1 on v0

--- a/solution.py
+++ b/solution.py
@@ -27,56 +27,56 @@
 
 
 PLANS[4] = (
-    (1, 1, 1, 1, 1, 1, 1, 1),
-    ((0, LINE), (0, LINE), (0, LINE), (1, HALF), (0, LINE), (0, LINE), (0, LINE), (0, LINE)),
-    ((1, LINE), (0, HALF), (0, HALF), (0, LINE), (1, LINE), (0, LINE), (0, LINE), (0, LINE)),
+    (3, 3, 3, 3, 2, 2),
     (
-        unpacked((
-            30, 1030, 103010, 103021, 103020, 6030, 103031, 4030, 20, 103030, 1020, 103011, 5030, 100030,
-            2030, 101030, 6020, 7030, 104030, 4020, 100020, 10, 101020, 106030, 105030, 5020, 203000, 0,
-            106020, 1010, 107030, 2020, 104020, 102030, 6010, 100010, 1000, 303000, 7020, 105020, 4010, 6000,
-            101010, 4000, 102020, 300000, 5010, 106010, 2010, 301000, 5000, 107020, 7010, 104010, 2000, 7000,
-            304000, 306000, 105010, 102010, 603110, 305000, 107010, 601110, 302000, 603130, 307000, 606120, 606110, 400000,
-            601130, 404000, 605110, 606130, 605120, 605130, 602120, 603120, 602130, 601120, 602110, 607130, 607120, 607110,
-        )),
-        unpacked((
-            30, 1030, 103110, 103111, 6030, 4030, 0, 20, 5030, 1000, 103011, 10, 103010, 1020,
-            103021, 103020, 2030, 203000, 6000, 101020, 6020, 100020, 1010, 104020, 7030, 100010, 4000, 101010,
-            303000, 101110, 4020, 105020, 100110, 6010, 106020, 4010, 106010, 5000, 5020, 107020, 503110, 2000,
-            300000, 104110, 2020, 102020, 104010, 106110, 5010, 7000, 503010, 7020, 301000, 105110, 500110, 2010,
-            105010, 7010, 102110, 306000, 500010, 102010, 503120, 603110, 501110, 304000, 107110, 107010, 506110, 606110,
-            506010, 606010, 603010, 305000, 500120, 302000, 501120, 601110, 505010, 605010, 307000, 506120, 504010, 601010,
-            505110, 605110, 505120, 602010, 502110, 602110, 507010, 502120, 400000, 504120, 606120, 500011, 507110, 504011,
-            602120, 507120, 605120, 500111, 603120, 404000, 500121, 601120, 504121, 607010, 607110, 504110, 504111, 607120,
-        )),
-        unpacked((
-            0, 1000, 103010, 103011, 6000, 4000, 30, 10, 5000, 1030, 103111, 20, 103110, 1010,
-            103121, 103120, 2000, 203000, 6030, 101120, 6010, 100120, 1020, 104120, 7000, 100110, 4030, 101110,
-            303000, 101010, 4010, 105120, 100010, 6020, 106120, 4020, 106110, 5030, 5010, 107120, 503010, 2030,
-            300000, 104010, 2010, 102120, 104110, 106010, 5020, 7030, 503110, 7010, 301000, 105010, 500010, 2020,
-            105110, 7020, 102010, 306000, 500110, 102110, 503020, 603010, 501010, 304000, 107010, 107110, 506010, 606010,
-            506110, 606110, 603110, 305000, 500020, 302000, 501020, 601010, 505110, 605110, 307000, 506020, 504110, 601110,
-            505010, 605010, 505020, 602110, 502010, 602010, 507110, 502020, 400000, 504020, 606020, 500111, 507010, 504111,
-            602020, 507020, 605020, 500011, 603020, 404000, 500021, 601020, 504021, 607110, 607010, 504010, 504011, 607020,
-        )),
-        unpacked((
-            0, 1000, 103110, 103121, 103120, 6000, 103131, 4000, 10, 103130, 1010, 103111, 5000, 100130,
-            2000, 101130, 6010, 7000, 104130, 4010, 100120, 20, 101120, 106130, 105130, 5010, 203000, 30,
-            106120, 1020, 107130, 2010, 104120, 102130, 6020, 100110, 1030, 303000, 7010, 105120, 4020, 6030,
-            101110, 4030, 102120, 300000, 5020, 106110, 2020, 301000, 5030, 107120, 7020, 104110, 2030, 7030,
-            304000, 306000, 105110, 102110, 603010, 305000, 107110, 601010, 302000, 603030, 307000, 606020, 606010, 400000,
-            601030, 404000, 605010, 606030, 605020, 605030, 602020, 603020, 602030, 601020, 602010, 607030, 607020, 607010,
-        )),
+        (
+            ((0, LINE), (0, DIRECT), (0, HALF), (0, HALF), (1, LINE), (1, LINE)),
+            ((0, LINE), (0, LINE), (1, HALF), (0, LINE), (0, HALF), (0, HALF)),
+            (
+                unpacked((
+                    30, 1030, 104010, 104031, 104030, 1020, 104021, 104020, 2030, 104011, 3030, 100030, 1010,
+                    101030, 2020, 101020, 3020, 105031, 2010, 103030, 105030, 3010, 101010, 1000, 105021, 204000,
+                    2000, 103020, 3000, 105020, 20, 103010, 105011, 301000, 10, 105010, 0, 303000, 100020,
+                    102030, 601110, 100010, 205000, 102020, 604110, 604120, 102010, 300000, 305000, 304000, 603110, 601130,
+                    601120, 302000, 603120, 603130, 605110, 605130, 600110, 402000, 600120, 605120, 604130, 600130,
+                )),
+                unpacked((
+                    30, 1030, 1000, 1020, 2030, 3030, 104021, 101020, 104020, 2000, 104011, 101110, 2020,
+                    104010, 104111, 3000, 100020, 3020, 104110, 101010, 204000, 1010, 102110, 2010, 103020, 105021,
+                    3010, 103110, 105020, 0, 304000, 301000, 103010, 20, 105011, 105111, 105010, 10, 105110,
+                    504110, 100110, 501010, 601010, 501110, 601110, 303000, 503010, 603010, 205000, 100010, 501120, 102020,
+                    503110, 603110, 102010, 601120, 503120, 603120, 300000, 305000, 500010, 505120, 302000, 605010, 504120,
+                    605120, 500110, 505110, 605110, 600010, 500120, 600110, 402000, 502110, 604110, 604010, 502120, 600120,
+                    604120, 502121, 502111,
+                )),
+                unpacked((
+                    0, 1000, 1030, 1010, 2000, 3000, 104121, 101120, 104120, 2030, 104111, 101010, 2010,
+                    104110, 104011, 3030, 100120, 3010, 104010, 101110, 204000, 1020, 102010, 2020, 103120, 105121,
+                    3020, 103010, 105120, 30, 304000, 301000, 103110, 10, 105111, 105011, 105110, 20, 105010,
+                    504010, 100010, 501110, 601110, 501010, 601010, 303000, 503110, 603110, 205000, 100110, 501020, 102120,
+                    503010, 603010, 102110, 601020, 503020, 603020, 300000, 305000, 500110, 505020, 302000, 605110, 504020,
+                    605020, 500010, 505010, 605010, 600110, 500020, 600010, 402000, 502010, 604010, 604110, 502020, 600020,
+                    604020, 502021, 502011,
+                )),
+                unpacked((
+                    0, 1000, 104110, 104131, 104130, 1010, 104121, 104120, 2000, 104111, 3000, 100130, 1020,
+                    101130, 2010, 101120, 3010, 105131, 2020, 103130, 105130, 3020, 101110, 1030, 105121, 204000,
+                    2030, 103120, 3030, 105120, 10, 103110, 105111, 301000, 20, 105110, 30, 303000, 100120,
+                    102130, 601010, 100110, 205000, 102120, 604010, 604020, 102110, 300000, 305000, 304000, 603010, 601030,
+                    601020, 302000, 603020, 603030, 605010, 605030, 600010, 402000, 600020, 605020, 604030, 600030,
+                )),
+            ),
+        ),
     ),
 )
 
 
 def plan_for(outer, owned):
     if outer in PLANS:
-        parts, sums, spreads, orders = PLANS[outer]
+        parts, turns = PLANS[outer]
         unit = owned // sum(parts)
         if unit * sum(parts) == owned and unit % 16 == 0:
-            return [unit * part for part in parts], sums, spreads, orders
+            return [unit * part for part in parts], turns
     orders = []
     for z in range(outer):
         order = [(ACROSS, 0, 0, (z + 1 + step) % outer, 0) for step in range(outer)]
@@ -93,18 +93,18 @@
                         order.append((PASS, 0, left, distance, 0))
                     order.append((OVER, 0, left, distance, 0))
         orders.append(order)
-    return [owned], [(0, LINE)], [(0, LINE)], orders
+    return [owned], [([(0, LINE)], [(0, LINE)], orders)]
 
 
 def kernel(
     outer, plan, grads, master, m_codes, m_scale, v_codes, v_scale,
     master_new, m_new, ms_new, v_new, vs_new, weights,
-    own, xgot, stage, right_got, left_got, ms_wide, vs_wide,
+    own, xgot, stage, right_got, left_got, one_kept, two_kept, ms_wide, vs_wide,
     master_in, m_in, v_in, ms_in, vs_in,
     own_sem, state_sem,
     x_send, x_recv, sum_send, right_recv, left_recv, first_send, pass_send, w_recv, a_send, a_recv,
 ):
-    sizes, sums, spreads, orders = plan
+    sizes, turns = plan
     pieces = len(sizes)
     starts = [sum(sizes[:k]) for k in range(pieces)]
     owned, width = master.shape[1], master.shape[2]
@@ -115,12 +115,15 @@
     place = lax.div(me, 2)
     other = place * 2 + 1 - x
 
+    forms = [form for sums, spreads, _ in turns for _, form in (*sums, *spreads)]
+    reach = outer - 1 if DIRECT in forms else max(1, outer - 2) if HALF in forms else 1
     barrier = pltpu.get_barrier_semaphore()
     pl.semaphore_signal(barrier, inc=1, device_id={"dp": other}, device_id_type=MESH)
-    for step in range(1, outer):
-        pl.semaphore_signal(
-            barrier, inc=1, device_id={"dp": lax.rem(place + step, outer) * 2 + x}, device_id_type=MESH
-        )
+    for step in range(1, reach + 1):
+        for near, inside in ((place - step, place >= step), (place + step, place + step < outer)):
+            pl.when(inside)(functools.partial(
+                pl.semaphore_signal, barrier, inc=1, device_id={"dp": near * 2 + x}, device_id_type=MESH
+            ))
 
     def rows_in(k):
         return pl.ds(starts[k], sizes[k])
@@ -129,25 +132,22 @@
         pltpu.make_async_copy(grads.at[:, rows_in(k), :], own.at[:, rows_in(k), :], own_sem.at[k])
         for k in range(pieces)
     ]
-    scale_copies = [
-        pltpu.make_async_copy(m_scale, ms_in, state_sem.at[3]),
-        pltpu.make_async_copy(v_scale, vs_in, state_sem.at[4]),
-    ]
     state_copies = [
         pltpu.make_async_copy(src, dst, state_sem.at[i])
-        for i, (src, dst) in enumerate(((master, master_in), (m_codes, m_in), (v_codes, v_in)))
+        for i, (src, dst) in enumerate((
+            (master, master_in), (m_codes, m_in), (v_codes, v_in), (m_scale, ms_in), (v_scale, vs_in),
+        ))
     ]
-    for copy in own_copies + scale_copies + state_copies:
+    uses = list(dict.fromkeys(step[1] for step in turns[0][2][0]))
+    for k in uses:
+        own_copies[k].start()
+    for copy in state_copies:
         copy.start()
-    for copy in scale_copies:
-        copy.wait()
-    for source, wide in ((ms_in, ms_wide), (vs_in, vs_wide)):
-        for c in range(owned // LANES):
-            span = pl.ds(c * LANES, LANES)
-            wide[span, :] = jnp.transpose(jnp.broadcast_to(source[0:1, span], (LANES, LANES)))
-    for copy in own_copies + state_copies:
-        copy.wait()
-    pl.semaphore_wait(barrier, outer)
+    near = sum(
+        (place >= step).astype(jnp.int32) + (place + step < outer).astype(jnp.int32)
+        for step in range(1, reach + 1)
+    )
+    pl.semaphore_wait(barrier, 1 + near)
 
     def remote(src, dst, send, recv, device):
         return pltpu.make_async_remote_copy(
@@ -171,9 +171,24 @@
         else:
             body(rows_in(k))
 
-    def program(z):
+    def program(turn, z):
+        sums, spreads, orders = turns[turn]
         started = []
         taken = set()
+        loaded = set()
+
+        def load(k):
+            if k not in loaded:
+                loaded.add(k)
+                own_copies[k].wait()
+
+        def load_state():
+            for copy in state_copies:
+                copy.wait()
+            for source, wide in ((ms_in, ms_wide), (vs_in, vs_wide)):
+                for c in range(owned // LANES):
+                    span = pl.ds(c * LANES, LANES)
+                    wide[span, :] = jnp.transpose(jnp.broadcast_to(source[0:1, span], (LANES, LANES)))
 
         def launch(copy):
             copy.start()
@@ -228,7 +243,12 @@
                     sum_wait(k, left, t, block)
 
                 def body(rows):
-                    total = add_up(k, t, block, [(left, t)] if adds else [], rows)
+                    if adds and z_first:
+                        total = own[t * 2 + column(block), rows, :] + got[t, block, rows, :]
+                    elif adds:
+                        total = add_up(k, t, block, [(left, t)], rows)
+                    else:
+                        total = own[t * 2 + column(block), rows, :] + xgot[t, rows, :]
                     stage[t, block, rows, :] = total.astype(bf16)
                 in_rows(k, body)
                 src = stage.at[t, block, rows_in(k), :]
@@ -317,6 +337,12 @@
                 mine = pl.ds(pl.multiple_of(me * owned + rows.start, 16), rows.size)
                 weights[0, mine, :] = new.astype(bf16)
                 master_new[0, rows] = new
+                one_kept[rows, :] = one
+                two_kept[rows, :] = two
+
+            def code(rows):
+                one = one_kept[rows, :]
+                two = two_kept[rows, :]
                 one_top = jnp.max(jnp.abs(one), axis=-1, keepdims=True) + 1e-06
                 two_top = jnp.max(jnp.abs(two), axis=-1, keepdims=True) + 1e-06
                 m_new[0, rows] = (one / one_top).astype(bf16)
@@ -329,6 +355,7 @@
             first_sends(k, 0)
             if not spreads[k][0]:
                 launch(weight_over(k, z))
+            in_rows(k, code)
 
         def spread(k):
             weight_over(k, z).wait_recv()
@@ -346,7 +373,15 @@
             weight_wait(k, source, 0)
             launch(weight_over(k, source))
 
+        ready = False
         for kind, k, left, distance, block in orders[z]:
+            load(k)
+            waits = kind > SUM or kind == SUM and (
+                not sums[k][0] or sums[k][1] != DIRECT and seat(left) > 0
+            )
+            if waits and not ready:
+                ready = True
+                load_state()
             if kind == ACROSS:
                 across(k, distance)
             elif kind == SUM:
@@ -375,8 +410,10 @@
                 if not spreads[k][0]:
                     weight_over(k, source).wait_recv()
 
-    for z in range(outer):
-        pl.when(place == z)(functools.partial(program, z))
+    shard = lax.rem(lax.axis_index("mp"), len(turns))
+    for turn in range(len(turns)):
+        for z in range(outer):
+            pl.when((place == z) & (shard == turn))(functools.partial(program, turn, z))
 
 
 def write_out(*refs):
@@ -395,9 +432,9 @@
     outer = lax.axis_size("dp") // 2
     _, owned, width = master.shape
     plan = plan_for(outer, owned)
-    sizes, sums, spreads, _ = plan
+    sizes, turns = plan
     pieces = len(sizes)
-    blocks = 1 + max(kind[0] for kind in (*sums, *spreads))
+    blocks = 1 + max(kind[0] for sums, spreads, _ in turns for kind in (*sums, *spreads))
     bf16, f32 = jnp.bfloat16, jnp.float32
     dma = pltpu.SemaphoreType.DMA
     shape = jax.ShapeDtypeStruct
@@ -419,6 +456,7 @@
             pltpu.VMEM((outer, blocks, owned, width), bf16),
             pltpu.VMEM((outer, blocks, owned, width), bf16),
             pltpu.VMEM((outer, blocks, owned, width), bf16),
+            pltpu.VMEM((owned, width), f32), pltpu.VMEM((owned, width), f32),
             pltpu.VMEM((owned, LANES), f32), pltpu.VMEM((owned, LANES), f32),
             pltpu.VMEM(state, f32), pltpu.VMEM(state, bf16), pltpu.VMEM(state, bf16),
             pltpu.VMEM((1, owned), f32), pltpu.VMEM((1, owned), f32),

time: 53.6 us -> 51.2 us (0.955)
  Pallas kernels: 52.9 us -> 50.4 us
    pallas_call x1, Pallas kernels: 51.1 us -> 48.7 us  [per_device(): pl.pallas_call(functools.partial(kernel, outer, plan), out_shape=tuple((p...]
where the time goes in v1:
time: 51.2 us; the launch traced here: 51.1 us
  Pallas kernels  50.4 us (98%)
  between operations  0.64 us (1%)
    pallas_call x1, Pallas kernels, per_device(): pl.pallas_call(functools.partial(kernel, outer, plan), out_shape=tuple((p...  48.7 us
    pallas_call x1, Pallas kernels, per_device(): pl.pallas_call(write_out, out_shape=tuple((shape(*each) for each in out_s...  1.73 us

profile of v1, /device:TPU:0, one launch (start us, length us, event | category | flops | bytes accessed | tf_op | source)
XLA Modules:
  0.0 51.1 jit_solution(3527692225134382493)
XLA Ops:
  0.6 48.7 %shard_map.109 = (f32[1,512,256]{2,1,0:T(8,128)S(1)}, bf16[1,512,256]{2,1,0:T(8,128)(2,1)S(1)}, f32[1,512]{1,0:T(1,128)S(1)}, bf16[1,512,256]{2,1,0:T(8,128)(2,1...) custom-call(bf16[8,512,256]{2,1,0:T(8,128)(2,1)} %bitcast.1, f32[1,512,256]{2,1,0:T(8,128)} %master.1, ...), custom_call_target="tpu_custom_call" | custom-call | tf_op jit(solution)/shard_map/pallas_call | solution.py:448
  49.4 1.7 %shard_map.110 = (f32[1,512,256]{2,1,0:T(8,128)}, bf16[1,512,256]{2,1,0:T(8,128)(2,1)}, f32[1,512]{1,0:T(1,128)}, bf16[1,512,256]{2,1,0:T(8,128)(2,1)}, f32[1,512]{1,0:T(1,128)}, /*index=5*/bf16[1,4096,256]{2,1,0:T(8,128)(2,1)}) custom-call(f32[1,512,256]{2,1,0:T(8,128)S(1)} %get-tuple-element.12.refs_0_, ...), custom_call_target="tpu_custom_call" | custom-call | tf_op jit(solution)/shard_map/pallas_call | solution.py:474

commit v2 on v1

--- a/solution.py
+++ b/solution.py
@@ -15,7 +15,8 @@
 MESH = pl.DeviceIdType.MESH
 
 LINE, HALF, DIRECT = 0, 1, 2
-ACROSS, SUM, CROSS, UPDATE, SPREAD, PASS, OVER = range(7)
+EACH, OWNER, INNER = 0, 1, 2
+ACROSS, SUM, CROSS, UPDATE, SPREAD, PASS, OVER, RELAY = range(8)
 CHUNK = 64
 PLANS = {}
 
@@ -30,40 +31,40 @@
     (3, 3, 3, 3, 2, 2),
     (
         (
-            ((0, LINE), (0, DIRECT), (0, HALF), (0, HALF), (1, LINE), (1, LINE)),
-            ((0, LINE), (0, LINE), (1, HALF), (0, LINE), (0, HALF), (0, HALF)),
+            ((0, LINE), (0, LINE), (0, HALF), (1, LINE), (0, HALF), (0, HALF)),
+            ((EACH, LINE), (EACH, LINE), (OWNER, LINE), (EACH, LINE), (EACH, LINE), (EACH, HALF)),
             (
                 unpacked((
-                    30, 1030, 104010, 104031, 104030, 1020, 104021, 104020, 2030, 104011, 3030, 100030, 1010,
-                    101030, 2020, 101020, 3020, 105031, 2010, 103030, 105030, 3010, 101010, 1000, 105021, 204000,
-                    2000, 103020, 3000, 105020, 20, 103010, 105011, 301000, 10, 105010, 0, 303000, 100020,
-                    102030, 601110, 100010, 205000, 102020, 604110, 604120, 102010, 300000, 305000, 304000, 603110, 601130,
-                    601120, 302000, 603120, 603130, 605110, 605130, 600110, 402000, 600120, 605120, 604130, 600130,
+                    30, 103010, 103031, 5030, 2030, 103030, 1030, 103021, 5020, 103020, 2020, 1020, 105030,
+                    103011, 5010, 2010, 101030, 4030, 105020, 100030, 1010, 4020, 101020, 4010, 105010, 102030,
+                    20, 203000, 104030, 10, 101010, 5000, 104020, 2000, 104010, 1000, 100020, 303000, 4000,
+                    100010, 102020, 0, 305000, 302000, 301000, 304000, 605110, 300000, 603120, 102010, 402000, 605120,
+                    601110, 604110, 605130, 603130, 601120, 604120, 603110, 600120, 601130, 604130, 600130, 600110,
                 )),
                 unpacked((
-                    30, 1030, 1000, 1020, 2030, 3030, 104021, 101020, 104020, 2000, 104011, 101110, 2020,
-                    104010, 104111, 3000, 100020, 3020, 104110, 101010, 204000, 1010, 102110, 2010, 103020, 105021,
-                    3010, 103110, 105020, 0, 304000, 301000, 103010, 20, 105011, 105111, 105010, 10, 105110,
-                    504110, 100110, 501010, 601010, 501110, 601110, 303000, 503010, 603010, 205000, 100010, 501120, 102020,
-                    503110, 603110, 102010, 601120, 503120, 603120, 300000, 305000, 500010, 505120, 302000, 605010, 504120,
-                    605120, 500110, 505110, 605110, 600010, 500120, 600110, 402000, 502110, 604110, 604010, 502120, 600120,
-                    604120, 502121, 502111,
+                    30, 5030, 2030, 1030, 5000, 5020, 2000, 103021, 2020, 103020, 1000, 103011, 1020,
+                    105110, 103010, 103111, 4030, 105020, 4000, 103110, 102110, 203000, 101020, 4020, 105010, 0,
+                    100020, 20, 101010, 5010, 104110, 101110, 303000, 102020, 2010, 104020, 1010, 100110, 4010,
+                    104010, 10, 305000, 503110, 100010, 603110, 503010, 301000, 505110, 605110, 304000, 300000, 102010,
+                    503120, 505120, 605120, 501010, 501110, 504010, 604010, 603120, 604110, 504110, 500010, 502010, 500110,
+                    605010, 302000, 502011, 501120, 601120, 604120, 504120, 601010, 500120, 601110, 603010, 402000, 502120,
+                    600120, 502121, 600010, 502110, 600110, 502111,
                 )),
                 unpacked((
-                    0, 1000, 1030, 1010, 2000, 3000, 104121, 101120, 104120, 2030, 104111, 101010, 2010,
-                    104110, 104011, 3030, 100120, 3010, 104010, 101110, 204000, 1020, 102010, 2020, 103120, 105121,
-                    3020, 103010, 105120, 30, 304000, 301000, 103110, 10, 105111, 105011, 105110, 20, 105010,
-                    504010, 100010, 501110, 601110, 501010, 601010, 303000, 503110, 603110, 205000, 100110, 501020, 102120,
-                    503010, 603010, 102110, 601020, 503020, 603020, 300000, 305000, 500110, 505020, 302000, 605110, 504020,
-                    605020, 500010, 505010, 605010, 600110, 500020, 600010, 402000, 502010, 604010, 604110, 502020, 600020,
-                    604020, 502021, 502011,
+                    0, 5000, 2000, 1000, 5030, 5010, 2030, 103121, 2010, 103120, 1030, 103111, 1010,
+                    105010, 103110, 103011, 4000, 105120, 4030, 103010, 102010, 203000, 101120, 4010, 105110, 30,
+                    100120, 10, 101110, 5020, 104010, 101010, 303000, 102120, 2020, 104120, 1020, 100010, 4020,
+                    104110, 20, 305000, 503010, 100110, 603010, 503110, 301000, 505010, 605010, 304000, 300000, 102110,
+                    503020, 505020, 605020, 501110, 501010, 504110, 604110, 603020, 604010, 504010, 500110, 502110, 500010,
+                    605110, 302000, 502111, 501020, 601020, 604020, 504020, 601110, 500020, 601010, 603110, 402000, 502020,
+                    600020, 502021, 600110, 502010, 600010, 502011,
                 )),
                 unpacked((
-                    0, 1000, 104110, 104131, 104130, 1010, 104121, 104120, 2000, 104111, 3000, 100130, 1020,
-                    101130, 2010, 101120, 3010, 105131, 2020, 103130, 105130, 3020, 101110, 1030, 105121, 204000,
-                    2030, 103120, 3030, 105120, 10, 103110, 105111, 301000, 20, 105110, 30, 303000, 100120,
-                    102130, 601010, 100110, 205000, 102120, 604010, 604020, 102110, 300000, 305000, 304000, 603010, 601030,
-                    601020, 302000, 603020, 603030, 605010, 605030, 600010, 402000, 600020, 605020, 604030, 600030,
+                    0, 103110, 103131, 5000, 2000, 103130, 1000, 103121, 5010, 103120, 2010, 1010, 105130,
+                    103111, 5020, 2020, 101130, 4000, 105120, 100130, 1020, 4010, 101120, 4020, 105110, 102130,
+                    10, 203000, 104130, 20, 101110, 5030, 104120, 2030, 104110, 1030, 100120, 303000, 4030,
+                    100110, 102120, 30, 305000, 302000, 301000, 304000, 605010, 300000, 603020, 102110, 402000, 605020,
+                    601010, 604010, 605030, 603030, 601020, 604020, 603010, 600020, 601030, 604030, 600030, 600010,
                 )),
             ),
         ),
@@ -93,7 +94,7 @@
                         order.append((PASS, 0, left, distance, 0))
                     order.append((OVER, 0, left, distance, 0))
         orders.append(order)
-    return [owned], [([(0, LINE)], [(0, LINE)], orders)]
+    return [owned], [([(0, LINE)], [(EACH, LINE)], orders)]
 
 
 def kernel(
@@ -350,10 +351,10 @@
                 ms_wide[rows, :] = jnp.broadcast_to(one_top, (rows.size, LANES))
                 vs_wide[rows, :] = jnp.broadcast_to(two_top, (rows.size, LANES))
             in_rows(k, body)
-            if spreads[k][0]:
+            if spreads[k][0] == OWNER:
                 launch(weight_over(k, z))
             first_sends(k, 0)
-            if not spreads[k][0]:
+            if spreads[k][0] != OWNER:
                 launch(weight_over(k, z))
             in_rows(k, code)
 
@@ -372,6 +373,17 @@
             source = at(left, seat(left) - apart)
             weight_wait(k, source, 0)
             launch(weight_over(k, source))
+
+        def over_wait(k, source):
+            if (k, source) not in taken:
+                taken.add((k, source))
+                weight_over(k, source).wait_recv()
+
+        def relay(k, left, source):
+            over_wait(k, source)
+            launch(weight_copy(
+                k, source, 1, pass_send.at[k, source, 1], at(left, seat(left) + 1)
+            ))
 
         ready = False
         for kind, k, left, distance, block in orders[z]:
@@ -394,8 +406,10 @@
                 spread(k)
             elif kind == PASS:
                 pass_on(k, left, distance, block)
+            elif kind == OVER:
+                over(k, left, distance)
             else:
-                over(k, left, distance)
+                relay(k, left, distance)
         for wide, out in ((ms_wide, ms_new), (vs_wide, vs_new)):
             for c in range(owned // LANES):
                 span = pl.ds(c * LANES, LANES)
@@ -403,12 +417,15 @@
         for copy in started:
             copy.wait_send()
         for k in range(pieces):
+            crossing = spreads[k][0]
+            ends = crossing == INNER and z in (0, outer - 1)
             for source in range(outer):
-                for block in range(1 + spreads[k][0]):
-                    if source != z:
-                        weight_wait(k, source, block)
-                if not spreads[k][0]:
-                    weight_over(k, source).wait_recv()
+                if source != z:
+                    weight_wait(k, source, 0)
+                    if crossing == OWNER or ends:
+                        weight_wait(k, source, 1)
+                if crossing != OWNER and (source == z or not ends):
+                    over_wait(k, source)
 
     shard = lax.rem(lax.axis_index("mp"), len(turns))
     for turn in range(len(turns)):
@@ -434,7 +451,7 @@
     plan = plan_for(outer, owned)
     sizes, turns = plan
     pieces = len(sizes)
-    blocks = 1 + max(kind[0] for sums, spreads, _ in turns for kind in (*sums, *spreads))
+    blocks = 1 + max(min(kind[0], 1) for sums, spreads, _ in turns for kind in (*sums, *spreads))
     bf16, f32 = jnp.bfloat16, jnp.float32
     dma = pltpu.SemaphoreType.DMA
     shape = jax.ShapeDtypeStruct

time: 51.2 us -> 50.8 us (level)
  no operation moved by 1% of the time
where the time goes in v2:
time: 50.8 us; the launch traced here: 50.6 us
  Pallas kernels  50 us (98%)
  between operations  0.64 us (1%)
    pallas_call x1, Pallas kernels, per_device(): pl.pallas_call(functools.partial(kernel, outer, plan), out_shape=tuple((p...  48.2 us
    pallas_call x1, Pallas kernels, per_device(): pl.pallas_call(write_out, out_shape=tuple((shape(*each) for each in out_s...  1.73 us

profile of v2, /device:TPU:0, one launch (start us, length us, event | category | flops | bytes accessed | tf_op | source)
XLA Modules:
  0.0 50.6 jit_solution(5772613497913586367)
XLA Ops:
  0.6 48.2 %shard_map.109 = (f32[1,512,256]{2,1,0:T(8,128)S(1)}, bf16[1,512,256]{2,1,0:T(8,128)(2,1)S(1)}, f32[1,512]{1,0:T(1,128)S(1)}, bf16[1,512,256]{2,1,0:T(8,128)(2,1...) custom-call(bf16[8,512,256]{2,1,0:T(8,128)(2,1)} %bitcast.1, f32[1,512,256]{2,1,0:T(8,128)} %master.1, ...), custom_call_target="tpu_custom_call" | custom-call | tf_op jit(solution)/shard_map/pallas_call | solution.py:465
  48.9 1.7 %shard_map.110 = (f32[1,512,256]{2,1,0:T(8,128)}, bf16[1,512,256]{2,1,0:T(8,128)(2,1)}, f32[1,512]{1,0:T(1,128)}, bf16[1,512,256]{2,1,0:T(8,128)(2,1)}, f32[1,512]{1,0:T(1,128)}, /*index=5*/bf16[1,4096,256]{2,1,0:T(8,128)(2,1)}) custom-call(f32[1,512,256]{2,1,0:T(8,128)S(1)} %get-tuple-element.12.refs_0_, ...), custom_call_target="tpu_custom_call" | custom-call | tf_op jit(solution)/shard_map/pallas_call | solution.py:491

commit v3 on v2

--- a/solution.py
+++ b/solution.py
@@ -17,7 +17,7 @@
 LINE, HALF, DIRECT = 0, 1, 2
 EACH, OWNER, INNER = 0, 1, 2
 ACROSS, SUM, CROSS, UPDATE, SPREAD, PASS, OVER, RELAY = range(8)
-CHUNK = 64
+CHUNK = 48
 PLANS = {}
 
 

time: 50.8 us -> 50.8 us (level)
  no operation moved by 1% of the time
where the time goes in v3:
time: 50.8 us; the launch traced here: 50.6 us
  Pallas kernels  50 us (98%)
  between operations  0.64 us (1%)
    pallas_call x1, Pallas kernels, per_device(): pl.pallas_call(functools.partial(kernel, outer, plan), out_shape=tuple((p...  48.2 us
    pallas_call x1, Pallas kernels, per_device(): pl.pallas_call(write_out, out_shape=tuple((shape(*each) for each in out_s...  1.73 us

profile of v3, /device:TPU:0, one launch (start us, length us, event | category | flops | bytes accessed | tf_op | source)
XLA Modules:
  0.0 50.6 jit_solution(11034422570452373489)
XLA Ops:
  0.6 48.2 %shard_map.109 = (f32[1,512,256]{2,1,0:T(8,128)S(1)}, bf16[1,512,256]{2,1,0:T(8,128)(2,1)S(1)}, f32[1,512]{1,0:T(1,128)S(1)}, bf16[1,512,256]{2,1,0:T(8,128)(2,1...) custom-call(bf16[8,512,256]{2,1,0:T(8,128)(2,1)} %bitcast.1, f32[1,512,256]{2,1,0:T(8,128)} %master.1, ...), custom_call_target="tpu_custom_call" | custom-call | tf_op jit(solution)/shard_map/pallas_call | solution.py:465
  48.9 1.7 %shard_map.110 = (f32[1,512,256]{2,1,0:T(8,128)}, bf16[1,512,256]{2,1,0:T(8,128)(2,1)}, f32[1,512]{1,0:T(1,128)}, bf16[1,512,256]{2,1,0:T(8,128)(2,1)}, f32[1,512]{1,0:T(1,128)}, /*index=5*/bf16[1,4096,256]{2,1,0:T(8,128)(2,1)}) custom-call(f32[1,512,256]{2,1,0:T(8,128)S(1)} %get-tuple-element.12.refs_0_, ...), custom_call_target="tpu_custom_call" | custom-call | tf_op jit(solution)/shard_map/pallas_call | solution.py:491
